TPU v7x, 32 devices: a whole 2x2x4 slice. The times are simulated.
32 devices in a mesh: dp: 8 (over y, x, core), mp: 4 (over z).
Axes of the slice: x: 2, y: 2, z: 4, core: 2. Of those that a mesh axis runs over, the one named last changes fastest.
Arguments:
- tokens: bfloat16 [5120, 768], P('dp'), may hold values from -6 to 6
- segment_ids: int32 [8, 640], P('dp'), may hold values from 0 to 3, never falling along the last dimension, each value on 1 to 320 neighbouring positions
- token_types: int32 [8, 640], P('dp'), may hold values 0 or 1
- q_weight: bfloat16 [4, 768, 768], P(None, None, 'mp'), may hold values from -0.21875 to 0.21875
- k_weight: bfloat16 [768, 768], P(None, 'mp'), may hold values from -0.21875 to 0.21875
- v_weight: bfloat16 [768, 768], P(None, 'mp'), may hold values from -0.21875 to 0.21875
- o_weight: bfloat16 [768, 768], P('mp'), may hold values from -2.5 to 2.5
- o_bias: float32 [768], replicated, may hold values from -1.5 to 1.5
- norm1_gain: float32 [768], replicated, may hold values from 0.25 to 1.75
- norm1_shift: float32 [768], replicated, may hold values from -1.5 to 1.5
- in_weight: bfloat16 [768, 3072], P(None, 'mp'), may hold values from -0.21875 to 0.21875
- in_bias: float32 [3072], P('mp'), may hold values from -1.5 to 1.5
- out_weight: bfloat16 [3072, 768], P('mp'), may hold values from -0.109375 to 0.109375
- out_bias: float32 [768], replicated, may hold values from -1.5 to 1.5
- norm2_gain: float32 [768], replicated, may hold values from 0.25 to 1.75
- norm2_shift: float32 [768], replicated, may hold values from -1.5 to 1.5
- cotangent: bfloat16 [5120, 768], P('dp'), may hold values from -6 to 6
Outputs:
- layer_out: bfloat16 [5120, 768], P('dp')
- tokens_grad: bfloat16 [5120, 768], P('dp')
- q_grad: float32 [4, 768, 768], P(None, 'dp', 'mp')
- k_grad: float32 [768, 768], P('dp', 'mp')
- v_grad: float32 [768, 768], P('dp', 'mp')
- o_grad: float32 [768, 768], P('mp', 'dp')
- o_bias_grad: float32 [768], replicated
- norm1_gain_grad: float32 [768], replicated
- norm1_shift_grad: float32 [768], replicated
- in_grad: float32 [768, 3072], P('dp', 'mp')
- in_bias_grad: float32 [3072], P('mp')
- out_grad: float32 [3072, 768], P('mp', 'dp')
- out_bias_grad: float32 [768], replicated
- norm2_gain_grad: float32 [768], replicated
- norm2_shift_grad: float32 [768], replicated
Inputs may be any that keep to these rules, and one draw needn't show every extreme that they name: `segment_ids`: a sequence's rows with equal ids form one run.
All inputs are finite; a program needn't handle non-finite values. No bound on the sum of `token_types` on one device may be relied on, other than what follows from the above.
Results may differ from a plain program's by a relative error of at most 0.019.
Values may be sent and summed in bfloat16 or wider, within the bound.
A program may use at most 128 MiB of HBM per device.

v0:
```python
import jax
import jax.numpy as jnp
from jax import lax
from jax.sharding import PartitionSpec as P

HD = 64
norm_epsilon = 1e-05


def layer_norm(inputs, gain, shift):
    average = jnp.mean(inputs, axis=-1, keepdims=True)
    centred = inputs - average
    spread = jnp.mean(centred * centred, axis=-1, keepdims=True)
    return centred * lax.rsqrt(spread + norm_epsilon) * gain + shift


def gelu_exact(inputs):
    return jax.nn.gelu(inputs, approximate=False)


def matmul(left, right):
    return jnp.dot(left, right, preferred_element_type=jnp.float32)


def local(
    tokens,
    segment_ids,
    token_types,
    q_weight,
    k_weight,
    v_weight,
    o_weight,
    o_bias,
    norm1_gain,
    norm1_shift,
    in_weight,
    in_bias,
    out_weight,
    out_bias,
    norm2_gain,
    norm2_shift,
    cotangent,
):
    row_count = tokens.shape[0]
    groups, length = segment_ids.shape
    local_width = k_weight.shape[1]
    head_count = local_width // HD
    score_scale = HD ** (-0.5)
    entity = token_types == 1
    chooser = entity[:, :, None, None]
    key_entity = entity[:, None, None, :]
    same_doc = (segment_ids[:, :, None] == segment_ids[:, None, :])[:, None]
    share_rows = row_count // lax.axis_size("mp")
    row_offset = lax.axis_index("mp") * share_rows
    queries = jnp.einsum(
        "rd,tdc->trc", tokens, q_weight, preferred_element_type=jnp.float32
    ).astype(jnp.bfloat16)
    keys = matmul(tokens, k_weight).astype(jnp.bfloat16)
    values = matmul(tokens, v_weight).astype(jnp.bfloat16)
    query_four = queries.reshape(4, groups, length, head_count, HD)
    query_word = jnp.where(chooser, query_four[2], query_four[0])
    query_ent = jnp.where(chooser, query_four[3], query_four[1])
    key_heads = keys.reshape(groups, length, head_count, HD)
    value_heads = values.reshape(groups, length, head_count, HD)

    def scores_now():
        raw_word = jnp.einsum(
            "gqhc,gkhc->ghqk", query_word, key_heads, preferred_element_type=jnp.float32
        )
        raw_ent = jnp.einsum(
            "gqhc,gkhc->ghqk", query_ent, key_heads, preferred_element_type=jnp.float32
        )
        raw_all = jnp.where(key_entity, raw_ent, raw_word)
        return jnp.where(same_doc, raw_all * score_scale, -1000000000.0)

    scores = scores_now()
    highest = jnp.max(scores, axis=-1, keepdims=True)
    log_total = highest + jnp.log(jnp.sum(jnp.exp(scores - highest), axis=-1, keepdims=True))
    attention_low = jnp.exp(scores - log_total).astype(jnp.bfloat16)
    mixed = jnp.einsum(
        "ghqk,gkhc->gqhc", attention_low, value_heads, preferred_element_type=jnp.float32
    )
    mixed = mixed.reshape(row_count, local_width).astype(jnp.bfloat16)
    token_wide = tokens.astype(jnp.float32)
    branch = lax.psum(matmul(mixed, o_weight), "mp") + o_bias
    hidden, norm1_pull = jax.vjp(layer_norm, token_wide + branch, norm1_gain, norm1_shift)
    hidden_low = hidden.astype(jnp.bfloat16)
    inner_pre = matmul(hidden_low, in_weight) + in_bias
    activated, gelu_pull = jax.vjp(gelu_exact, inner_pre)
    activated_low = activated.astype(jnp.bfloat16)
    ffn_out = (
        lax.psum(matmul(activated_low, out_weight).astype(jnp.bfloat16), "mp").astype(jnp.float32)
        + out_bias
    )
    result, norm2_pull = jax.vjp(layer_norm, hidden + ffn_out, norm2_gain, norm2_shift)
    layer_out = result.astype(jnp.bfloat16)
    d_res2, d_gain2, d_shift2 = norm2_pull(cotangent.astype(jnp.float32))
    d_out_bias = jnp.sum(d_res2, axis=0)
    grad_ffn = d_res2.astype(jnp.bfloat16)
    d_out_weight = matmul(activated_low.T, grad_ffn)
    (d_inner,) = gelu_pull(matmul(grad_ffn, out_weight.T))
    d_in_bias = jnp.sum(d_inner, axis=0)
    inner_low = d_inner.astype(jnp.bfloat16)
    d_in_weight = matmul(hidden_low.T, inner_low)
    d_hidden = d_res2 + lax.psum(matmul(inner_low, in_weight.T).astype(jnp.bfloat16), "mp").astype(
        jnp.float32
    )
    d_res1, d_gain1, d_shift1 = norm1_pull(d_hidden)
    d_o_bias = jnp.sum(d_res1, axis=0)
    grad_branch = d_res1.astype(jnp.bfloat16)
    d_o_weight = matmul(mixed.T, grad_branch)
    d_mixed = matmul(grad_branch, o_weight.T).astype(jnp.bfloat16)
    mixed_heads = d_mixed.reshape(groups, length, head_count, HD)
    attention = jnp.exp(scores_now() - log_total)
    d_probs = jnp.einsum(
        "gqhc,gkhc->ghqk", mixed_heads, value_heads, preferred_element_type=jnp.float32
    )
    d_values = jnp.einsum(
        "ghqk,gqhc->gkhc",
        attention.astype(jnp.bfloat16),
        mixed_heads,
        preferred_element_type=jnp.float32,
    )
    row_delta = jnp.sum(attention * d_probs, axis=-1, keepdims=True)
    d_raw = (attention * (d_probs - row_delta) * score_scale).astype(jnp.bfloat16)
    nothing = jnp.zeros_like(d_raw)
    raw_word = jnp.where(key_entity, nothing, d_raw)
    raw_ent = jnp.where(key_entity, d_raw, nothing)
    d_query_word = jnp.einsum(
        "ghqk,gkhc->gqhc", raw_word, key_heads, preferred_element_type=jnp.float32
    )
    d_query_ent = jnp.einsum(
        "ghqk,gkhc->gqhc", raw_ent, key_heads, preferred_element_type=jnp.float32
    )
    d_keys = jnp.einsum(
        "ghqk,gqhc->gkhc", raw_word, query_word, preferred_element_type=jnp.float32
    ) + jnp.einsum("ghqk,gqhc->gkhc", raw_ent, query_ent, preferred_element_type=jnp.float32)
    empty_rows = jnp.zeros_like(d_query_word)
    d_queries = (
        jnp.stack(
            [
                jnp.where(chooser, empty_rows, d_query_word),
                jnp.where(chooser, empty_rows, d_query_ent),
                jnp.where(chooser, d_query_word, empty_rows),
                jnp.where(chooser, d_query_ent, empty_rows),
            ]
        )
        .reshape(4, row_count, local_width)
        .astype(jnp.bfloat16)
    )
    d_keys_low = d_keys.reshape(row_count, local_width).astype(jnp.bfloat16)
    d_values_low = d_values.reshape(row_count, local_width).astype(jnp.bfloat16)
    d_q_weight = jnp.einsum("rd,trc->tdc", tokens, d_queries, preferred_element_type=jnp.float32)
    d_k_weight = matmul(tokens.T, d_keys_low)
    d_v_weight = matmul(tokens.T, d_values_low)
    res_rows = lax.dynamic_slice_in_dim(d_res1, row_offset, share_rows, 0)
    total = jnp.einsum("trc,tdc->rd", d_queries, q_weight, preferred_element_type=jnp.float32)
    grad_rows = (
        res_rows
        + lax.psum_scatter(
            (total + matmul(d_keys_low, k_weight.T) + matmul(d_values_low, v_weight.T)).astype(
                jnp.bfloat16
            ),
            "mp",
            scatter_dimension=0,
            tiled=True,
        ).astype(jnp.float32)
    ).astype(jnp.bfloat16)
    tokens_grad = lax.all_gather(grad_rows, "mp", axis=0, tiled=True)
    d_q_weight, d_k_weight, d_v_weight, d_o_weight, d_in_weight, d_out_weight = (
        lax.psum_scatter(d_q_weight, "dp", scatter_dimension=1, tiled=True),
        lax.psum_scatter(d_k_weight, "dp", scatter_dimension=0, tiled=True),
        lax.psum_scatter(d_v_weight, "dp", scatter_dimension=0, tiled=True),
        lax.psum_scatter(d_o_weight, "dp", scatter_dimension=1, tiled=True),
        lax.psum_scatter(d_in_weight, "dp", scatter_dimension=0, tiled=True),
        lax.psum_scatter(d_out_weight, "dp", scatter_dimension=1, tiled=True),
    )
    d_o_bias, d_gain1, d_shift1, d_in_bias, d_out_bias, d_gain2, d_shift2 = lax.psum(
        (d_o_bias, d_gain1, d_shift1, d_in_bias, d_out_bias, d_gain2, d_shift2), "dp"
    )
    return (
        layer_out,
        tokens_grad,
        d_q_weight,
        d_k_weight,
        d_v_weight,
        d_o_weight,
        d_o_bias,
        d_gain1,
        d_shift1,
        d_in_weight,
        d_in_bias,
        d_out_weight,
        d_out_bias,
        d_gain2,
        d_shift2,
    )


def solution(mesh):
    return jax.shard_map(
        local,
        mesh=mesh,
        in_specs=(
            P("dp", None),
            P("dp", None),
            P("dp", None),
            P(None, None, "mp"),
            P(None, "mp"),
            P(None, "mp"),
            P("mp", None),
            P(),
            P(),
            P(),
            P(None, "mp"),
            P("mp"),
            P("mp", None),
            P(),
            P(),
            P(),
            P("dp", None),
        ),
        out_specs=(
            P("dp", None),
            P("dp", None),
            P(None, "dp", "mp"),
            P("dp", "mp"),
            P("dp", "mp"),
            P("mp", "dp"),
            P(),
            P(),
            P(),
            P("dp", "mp"),
            P("mp"),
            P("mp", "dp"),
            P(),
            P(),
            P(),
        ),
        check_vma=False,
    )
```

profile of v0, /device:TPU:0, one launch (start us, length us, event | category | flops | bytes accessed | tf_op | source)
XLA Modules:
  0.0 547.0 jit_solution(5020968630286662695)
XLA Ops:
  8.1 1.7 convolution_convert_fusion.6
  9.9 1.8 convolution_convert_fusion.7
  12.0 2.4 fusion.19
  15.5 1.6 fusion.77
  17.8 1.5 copy-done.2
  20.3 1.8 fusion.81
  22.2 84.7 %all-reduce.5.cloned.1.call-done = f32[640,768]{1,0:T(8,128)} async-done(((f32[640,768]{1,0:T(8,128)}), f32[640,768]{1,0:T(8,128)}) %all-reduce.5.cloned.1.call-update) | async-done | bytes 1966096 | tf_op jit(solution)/shard_map/psum | solution.py:85
  106.9 2.1 fusion.75
  109.7 6.5 %multiply_convert_fusion.1 = (bf16[640,768]{1,0:T(8,128)(2,1)S(1)}, f32[640,768]{1,0:T(8,128)}, f32[640,768]{1,0:T(8,128)}) fusion(f32[768]{0:T(1024)S(1)} %copy-done.36, bf16[768,768]{1,0:T(8,128)(2,1)S(1)} %copy-done, f32[640,768]{1,0:T(8,128)S(1)} %get-tuple-element.70, f32[768]{0:T(1024)S(1)} %copy-done.31, f32[768]{0:T(1024)S(1)} %copy-done.27, ...), kind=kOutput, calls=%fused_computation.32 | convolution fusion | flops 789872640 | bytes 8075264 | tf_op jit(solution)/shard_map/dot_general | solution.py:22
  116.2 1.0 copy-done.39
  117.2 1.9 convolution_convert_fusion.1
  119.6 48.5 %all-reduce.7.cloned.1.call-done = bf16[640,768]{1,0:T(8,128)(2,1)} async-done(((bf16[640,768]{1,0:T(8,128)(2,1)}), bf16[640,768]{1,0:T(8,128)(2,1)}) %all-reduce.7.cloned.1.call-update) | async-done | bytes 983056 | tf_op jit(solution)/shard_map/psum | solution.py:92
  168.2 1.9 fusion.73
  172.2 1.8 fusion.72
  175.1 1.5 fusion.80
  177.6 1.9 convolution_convert_fusion
  179.6 49.1 %all-reduce.9.cloned.1.call-done = bf16[640,768]{1,0:T(8,128)(2,1)} async-done(((bf16[640,768]{1,0:T(8,128)(2,1)}), bf16[640,768]{1,0:T(8,128)(2,1)}) %all-reduce.9.cloned.1.call-update) | async-done | bytes 983056 | tf_op jit(solution)/shard_map/psum | solution.py:105
  228.7 3.1 multiply_reduce_fusion.1
  231.8 1.0 fusion.71
  234.5 1.5 convolution_bitcast_fusion.1
  235.9 3.4 convolution_convert_fusion.3
  239.3 3.1 fusion.82
  242.4 9.7 %fusion.21 = f32[3,64,640]{2,1,0:T(8,128)} fusion(pred[640]{0:T(1024)(128)(4,1)S(1)} %compare_reduce_fusion, f32[3,640,640]{1,2,0:T(8,128)} %fusion.82, f32[3,640,640]{1,2,0:T(8,128)} %copy-done.2, f32[3,640]{1,0:T(4,128)S(1)} %log_add_fusion, bf16[640,3,64]{0,2,1:T(8,128)(2,1)S(1)} %bitcast.122, bf16[640,3,64]{0,2,1:T(8,128)(2,1)S(1)} %bitcast.120), kind=kOutput, calls=%fused_computation.69 | convolution fusion | flops 167242240 | bytes 10821760 | tf_op jit(solution)/shard_map/ghqk,gqhc->gkhc/dot_general | solution.py:135
  252.1 9.6 %convolution_bitcast_fusion.4 = bf16[1,3,64,640]{3,2,1,0:T(8,128)(2,1)} fusion(bf16[640,3,64]{0,2,1:T(8,128)(2,1)S(1)} %bitcast.104, pred[640]{0:T(1024)(128)(4,1)S(1)} %compare_reduce_fusion, f32[3,640,640]{1,2,0:T(8,128)} %fusion.82, f32[3,640,640]{1,2,0:T(8,128)} %copy-done.2, f32[3,640]{1,0:T(4,128)S(1)} %log_add_fusion), kind=kOutput, calls=%fused_computation.60 | convolution fusion | flops 167119360 | bytes 10330240 | tf_op jit(solution)/shard_map/ghqk,gkhc->gqhc/dot_general | solution.py:132
  261.9 1.7 fusion.84
  263.7 9.3 %fusion.20 = bf16[3,64,640]{2,1,0:T(8,128)(2,1)S(1)} fusion(f32[3,64,640]{2,1,0:T(8,128)} %fusion.21, pred[640]{0:T(1024)(128)(4,1)S(1)} %compare_reduce_fusion, f32[3,640,640]{1,2,0:T(8,128)} %fusion.82, f32[3,640,640]{1,2,0:T(8,128)} %copy-done.2, f32[3,640]{1,0:T(4,128)S(1)} %log_add_fusion, bf16[640,3,64]{0,2,1:T(8,128)(2,1)} %bitcast.118, ...), kind=kOutput, calls=%fused_computation.63 | convolution fusion | flops 167488000 | bytes 11067520 | tf_op jit(solution)/shard_map/ghqk,gqhc->gkhc/dot_general | solution.py:137
  272.9 9.9 %select_convert_fusion.3 = (bf16[1,3,64,640]{3,2,1,0:T(8,128)(2,1)}, bf16[1,3,64,640]{3,2,1,0:T(8,128)(2,1)}, bf16[1,3,64,640]{3,2,1,0:T(8,128)(2,1)}, bf16[1,3,64,640]{3,2,1,0:T(8,128)(2,1)}) fusion(pred[640]{0:T(1024)(128)(4,1)S(1)} %compare_reduce_fusion, bf16[1,3,64,640]{3,2,1,0:T(8,128)(2,1)} %convolution_bitcast_fusion.4, ...), kind=kOutput, calls=%fused_computation.79 | convolution fusion | flops 167610880 | bytes 11313280 | tf_op jit(solution)/shard_map/ghqk,gkhc->gqhc/dot_general | solution.py:129
  283.4 1.0 copy-done.14
  284.5 3.6 fusion.12
  288.2 3.9 convolution_bitcast_fusion
  292.1 4.5 copy.56
  296.6 4.7 reshape.292
  301.4 1.2 convolution_bitcast_fusion.2
  302.6 2.2 copy.60
  304.9 2.2 convolution_bitcast_fusion.3
  307.1 2.4 copy.58
  309.6 4.2 fusion.64
  315.0 2.8 fusion.44
  317.8 24.7 %all-reduce = (f32[768]{0:T(1024)}, f32[768]{0:T(1024)}, f32[768]{0:T(1024)}, f32[768]{0:T(1024)}, f32[768]{0:T(1024)}, /*index=5*/f32[768]{0:T(1024)}, f32[768]{0:T(1024)}) all-reduce(f32[768]{0:T(1024)S(1)} %get-tuple-element.59, f32[768]{0:T(1024)S(1)} %get-tuple-element.45, ...), channel_id=1, replica_groups=mesh['dp'=8,'mp'=4] {'dp'}, use_global_device_ids=true, to_apply=%region_20.21 | all-reduce | flops 5376 | bytes 43008 | tf_op jit(solution)/shard_map/psum | solution.py:178
  342.5 1.6 copy.63
  344.1 1.2 add_convert_fusion.2
  345.3 19.9 %all_gather.3 = bf16[640,768]{1,0:T(8,128)(2,1)S(1)} all-gather(bf16[160,768]{1,0:T(8,128)(2,1)S(1)} %add_convert_fusion.2), channel_id=1, replica_groups=mesh['dp'=8,'mp'=4] {'mp'}, dimensions={0}, use_global_device_ids=true | all-gather | bytes 1228800 | tf_op jit(solution)/shard_map/all_gather | solution.py:169
  365.2 3.9 reduce-scatter.22.cloned.1.call-done
  369.2 1.2 reshape.293
  371.2 36.6 %reduce-scatter.26.cloned.1.call-done = f32[96,192]{1,0:T(8,128)} async-done(((f32[768,192]{1,0:T(8,128)}), f32[96,192]{1,0:T(8,128)}) %reduce-scatter.26.cloned.1.call-update) | async-done | bytes 73744
  407.8 38.7 %reduce-scatter.24.cloned.1.call-done = f32[96,192]{1,0:T(8,128)} async-done(((f32[768,192]{1,0:T(8,128)}), f32[96,192]{1,0:T(8,128)}) %reduce-scatter.24.cloned.1.call-update) | async-done | bytes 73744
  446.5 46.3 %reduce-scatter.20.cloned.1.call-done = f32[768,96]{0,1:T(8,128)} async-done(((f32[768,768]{0,1:T(8,128)}), f32[768,96]{0,1:T(8,128)}) %reduce-scatter.20.cloned.1.call-update) | async-done | bytes 294928 | tf_op jit(solution)/shard_map/reduce_scatter | solution.py:176
  492.8 46.1 %reduce-scatter.18.cloned.1.call-done = f32[96,768]{1,0:T(8,128)} async-done(((f32[768,768]{1,0:T(8,128)}), f32[96,768]{1,0:T(8,128)}) %reduce-scatter.18.cloned.1.call-update) | async-done | bytes 294928 | tf_op jit(solution)/shard_map/reduce_scatter | solution.py:175
  (133 shorter events, 14.9 us)
Async XLA Ops:
  7.2 102.2 %copy-start = (bf16[768,768]{1,0:T(8,128)(2,1)S(1)}, bf16[768,768]{1,0:T(8,128)(2,1)}, u32[]{:S(2)}) copy-start(bf16[768,768]{1,0:T(8,128)(2,1)} %param.27) | copy-start | bytes 3538948
  7.2 4.8 copy-start.3
  7.2 4.5 copy-start.33
  7.2 99.6 %all-reduce.5.cloned.1.call-start = ((), (), s32[]{:S(2)}) async-start(), calls=%async_computation.7 | async-start | bytes 3932160 | tf_op jit(solution)/shard_map/psum | solution.py:85
  9.8 5.6 %copy-start.10 = (bf16[640,192]{0,1:T(8,128)(2,1)}, bf16[640,192]{0,1:T(8,128)(2,1)S(1)}, u32[]{:S(2)}) copy-start(bf16[640,192]{0,1:T(8,128)(2,1)S(1)} %convolution_convert_fusion.6) | copy-start | bytes 737284
  11.7 6.1 %copy-start.12 = (bf16[640,192]{0,1:T(8,128)(2,1)}, bf16[640,192]{0,1:T(8,128)(2,1)S(1)}, u32[]{:S(2)}) copy-start(bf16[640,192]{0,1:T(8,128)(2,1)S(1)} %convolution_convert_fusion.7) | copy-start | bytes 737284
  17.1 2.2 copy-start.2
  19.3 1.0 copy-start.15
  20.3 86.6 %copy-start.29 = (f32[768]{0:T(1024)S(1)}, f32[768]{0:T(1024)}, u32[]{:S(2)}) copy-start(f32[768]{0:T(1024)} %param.24) | copy-start | bytes 9220
  22.1 146.0 %all-reduce.7.cloned.1.call-start = ((), (), s32[]{:S(2)}) async-start(), calls=%async_computation.8 | async-start | bytes 1966080 | tf_op jit(solution)/shard_map/psum | solution.py:92
  109.7 7.5 %copy-start.34 = (bf16[768,768]{1,0:T(8,128)(2,1)S(1)}, bf16[768,768]{1,0:T(8,128)(2,1)}, u32[]{:S(2)}) copy-start(bf16[768,768]{1,0:T(8,128)(2,1)} %param.29) | copy-start | bytes 3538948
  116.2 1.0 copy-start.39
  117.2 50.9 %copy-start.30 = (f32[768]{0:T(1024)S(1)}, f32[768]{0:T(1024)}, u32[]{:S(2)}) copy-start(f32[768]{0:T(1024)} %param.30) | copy-start | bytes 9220
  119.1 109.6 %all-reduce.9.cloned.1.call-start = ((), (), s32[]{:S(2)}) async-start(), calls=%async_computation.9 | async-start | bytes 1966080 | tf_op jit(solution)/shard_map/psum | solution.py:105
  170.1 1.2 copy-start.9
  170.1 1.2 copy-start.28
  170.5 1.7 copy-start.32
  172.2 1.9 copy-start.35
  172.2 2.0 copy-start.43
  172.2 2.9 copy-start.44
  174.0 2.6 copy-start.6
  176.6 1.0 copy-start.41
  179.5 163.0 %reduce-scatter.28.cloned.1.call-start = ((), (), s32[]{:S(2)}) async-start(), calls=%async_computation.16 | async-start | bytes 884736
  228.7 3.1 copy-start.7
  228.7 3.1 copy-start.8
  232.8 1.0 copy-start.16
  233.1 1.4 copy-start.5
  235.9 3.4 copy-start.13
  239.3 3.1 copy-start.24
  239.3 3.1 copy-start.26
  242.4 9.7 %copy-start.11 = (bf16[640,192]{0,1:T(8,128)(2,1)S(1)}, bf16[640,192]{0,1:T(8,128)(2,1)}, u32[]{:S(2)}) copy-start(bf16[640,192]{0,1:T(8,128)(2,1)} %copy-done.10) | copy-start | bytes 737284
  252.1 9.8 %copy-start.17 = (bf16[768,192]{0,1:T(8,128)(2,1)S(1)}, bf16[768,192]{0,1:T(8,128)(2,1)}, u32[]{:S(2)}) copy-start(bf16[768,192]{0,1:T(8,128)(2,1)} %param.22) | copy-start | bytes 884740
  261.7 2.0 copy-start.21
  261.7 82.4 %reduce-scatter.16.cloned.1.call-start = ((), (), s32[]{:S(2)}) async-start(), calls=%async_computation.10 | async-start | bytes 1228800 | tf_op jit(solution)/shard_map/reduce_scatter | solution.py:160
  272.9 9.9 %copy-start.19 = (bf16[3,64,640]{2,1,0:T(8,128)(2,1)}, bf16[3,64,640]{2,1,0:T(8,128)(2,1)S(1)}, u32[]{:S(2)}) copy-start(bf16[3,64,640]{2,1,0:T(8,128)(2,1)S(1)} %fusion.20) | copy-start | bytes 737284
  272.9 9.9 %copy-start.18 = (bf16[768,192]{0,1:T(8,128)(2,1)S(1)}, bf16[768,192]{0,1:T(8,128)(2,1)}, u32[]{:S(2)}) copy-start(bf16[768,192]{0,1:T(8,128)(2,1)} %param.21) | copy-start | bytes 884740
  282.9 1.5 copy-start.14
  282.9 1.5 copy-start.37
  282.9 1.6 copy-start.38
  284.5 3.7 copy-start.4
  288.1 81.0 %reduce-scatter.22.cloned.1.call-start = ((), (), s32[]{:S(2)}) async-start(), calls=%async_computation.13 | async-start | bytes 2654208
  301.3 106.5 %reduce-scatter.26.cloned.1.call-start = ((), (), s32[]{:S(2)}) async-start(), calls=%async_computation.15 | async-start | bytes 884736
  304.8 141.7 %reduce-scatter.24.cloned.1.call-start = ((), (), s32[]{:S(2)}) async-start(), calls=%async_computation.14 | async-start | bytes 884736
  307.1 2.4 copy-start.40
  309.5 183.3 %reduce-scatter.20.cloned.1.call-start = ((), (), s32[]{:S(2)}) async-start(), calls=%async_computation.12 | async-start | bytes 2654208 | tf_op jit(solution)/shard_map/reduce_scatter | solution.py:176
  313.8 1.2 copy-start.42
  313.8 225.2 %reduce-scatter.18.cloned.1.call-start = ((), (), s32[]{:S(2)}) async-start(), calls=%async_computation.11 | async-start | bytes 2654208 | tf_op jit(solution)/shard_map/reduce_scatter | solution.py:175
  345.3 194.6 %copy-start.1 = (bf16[768,768]{1,0:T(8,128)(2,1)S(1)}, bf16[768,768]{1,0:T(8,128)(2,1)}, u32[]{:S(2)}) copy-start(bf16[768,768]{1,0:T(8,128)(2,1)} %param.27) | copy-start | bytes 3538948
  (7 other events, 5.7 us)
Sparse Core Ops, SparseCore 0:
  22.2 84.5 all-reduce.4
  119.2 48.8 all-reduce.6
  179.6 49.0 all-reduce.8
  261.8 34.1 reduce-scatter.27
  298.7 26.2 reduce-scatter.15
  328.2 40.9 reduce-scatter.21
  372.9 34.9 reduce-scatter.25
  411.6 34.9 reduce-scatter.23
  450.5 42.3 reduce-scatter.19
  496.6 42.3 reduce-scatter.17
where the time goes:
time: 554 us; the launch traced here: 547 us
  waiting for transfers between devices  354 us (64%)
  matrix products  90 us (16%)
  blocking collectives  44.6 us (8%)
  local copies, waits for them, and re-layouts  27.3 us (5%)
  between operations  14.9 us (3%)
  other arithmetic  14.8 us (3%)
    psum x1, waiting for transfers between devices, local(): branch = lax.psum(matmul(mixed, o_weight), 'mp') + o_bias  84.7 us
    unnamed x14, waiting for transfers between devices  79.4 us
    psum x1, waiting for transfers between devices, local(): lax.psum(matmul(inner_low, in_weight.T).astype(jnp.bfloat16), 'mp')  49.1 us
    psum x1, waiting for transfers between devices, local(): lax.psum(matmul(activated_low, out_weight).astype(jnp.bfloat16), 'mp')  48.5 us
    reduce_scatter x1, waiting for transfers between devices, local(): lax.psum_scatter(d_out_weight, 'dp', scatter_dimension=1, tiled=True)  46.3 us
    reduce_scatter x1, waiting for transfers between devices, local(): lax.psum_scatter(d_in_weight, 'dp', scatter_dimension=0, tiled=True)  46.1 us
    dot_general x14, matrix products, matmul(): return jnp.dot(left, right, preferred_element_type=jnp.float32)  30.4 us
    unnamed x98, local copies, waits for them, and re-layouts  27.2 us
  transfers between devices with their start and end apart: 10, of which 8 were waited for; matrix products, arithmetic and copies ran while one was open for 11% of the time, Pallas kernels for 0%

commit v1 on v0

--- a/solution.py
+++ b/solution.py
@@ -5,6 +5,20 @@
 
 HD = 64
 norm_epsilon = 1e-05
+
+
+def _keep_up_inputs(tile_in, dev_axis):
+    even = jax.lax.psum(1, dev_axis)
+    tall = jax.lax.axis_index(dev_axis)
+    mid_arr, g_now, side_arr = (even, tall, tile_in.shape[0])
+    w1, z2 = (tile_in, 1)
+    while z2 < mid_arr:
+        v_next = jax.lax.ppermute(
+            w1, dev_axis, perm=[(pp, (pp - z2) % mid_arr) for pp in range(mid_arr)]
+        )
+        w1 = jnp.concatenate([w1, v_next], 0)
+        z2 = 2 * z2
+    return jnp.roll(w1, g_now * side_arr, 0)
 
 
 def layer_norm(inputs, gain, shift):
@@ -166,7 +180,7 @@
             tiled=True,
         ).astype(jnp.float32)
     ).astype(jnp.bfloat16)
-    tokens_grad = lax.all_gather(grad_rows, "mp", axis=0, tiled=True)
+    tokens_grad = _keep_up_inputs(grad_rows, "mp")
     d_q_weight, d_k_weight, d_v_weight, d_o_weight, d_in_weight, d_out_weight = (
         lax.psum_scatter(d_q_weight, "dp", scatter_dimension=1, tiled=True),
         lax.psum_scatter(d_k_weight, "dp", scatter_dimension=0, tiled=True),

time: 554 us -> 579 us (1.045)
  waiting for transfers between devices: 354 us -> 377 us
  blocking collectives: 44.6 us -> 23.7 us
  starting transfers between devices: 1.26 us -> 14.9 us
  local copies, waits for them, and re-layouts: 27.3 us -> 33.4 us
    unnamed x14, waiting for transfers between devices: 79.4 us -> 108 us
    all_gather x1 -> x0, blocking collectives: 19.9 us -> none  [local(): tokens_grad = lax.all_gather(grad_rows, 'mp', axis=0, tiled=True)]
    psum x1, waiting for transfers between devices: 48.5 us -> 37.2 us  [local(): lax.psum(matmul(activated_low, out_weight).astype(jnp.bfloat16), 'mp')]
    psum x1, starting transfers between devices: 0.51 us -> 11.8 us  [local(): lax.psum(matmul(inner_low, in_weight.T).astype(jnp.bfloat16), 'mp')]
    ppermute x0 -> x2, waiting for transfers between devices: none -> 6.16 us  [_keep_up_inputs(): jax.lax.ppermute(w1, dev_axis, perm=[(pp, (pp - z2) % mid_arr) for pp in...]
    unnamed x98 -> x103, local copies, waits for them, and re-layouts: 27.2 us -> 30 us
  transfers between devices with their start and end apart: 10 -> 12, of which waited for: 8 -> 9; matrix products, arithmetic and copies ran while one was open for 11% -> 8% of each run, Pallas kernels for 0% -> 0%
where the time goes in v1:
time: 579 us; the launch traced here: 571 us
  waiting for transfers between devices  377 us (65%)
  matrix products  88.9 us (15%)
  local copies, waits for them, and re-layouts  33.4 us (6%)
  blocking collectives  23.7 us (4%)
  other arithmetic  17.5 us (3%)
  between operations  15.1 us (3%)
  starting transfers between devices  14.9 us (3%)
    unnamed x14, waiting for transfers between devices  108 us
    psum x1, waiting for transfers between devices, local(): branch = lax.psum(matmul(mixed, o_weight), 'mp') + o_bias  84.7 us
    psum x1, waiting for transfers between devices, local(): lax.psum(matmul(inner_low, in_weight.T).astype(jnp.bfloat16), 'mp')  49.1 us
    reduce_scatter x1, waiting for transfers between devices, local(): lax.psum_scatter(d_out_weight, 'dp', scatter_dimension=1, tiled=True)  46.3 us
    reduce_scatter x1, waiting for transfers between devices, local(): lax.psum_scatter(d_in_weight, 'dp', scatter_dimension=0, tiled=True)  46.1 us
    psum x1, waiting for transfers between devices, local(): lax.psum(matmul(activated_low, out_weight).astype(jnp.bfloat16), 'mp')  37.2 us
    dot_general x14, matrix products, matmul(): return jnp.dot(left, right, preferred_element_type=jnp.float32)  30.3 us
    unnamed x103, local copies, waits for them, and re-layouts  30 us
  transfers between devices with their start and end apart: 12, of which 9 were waited for; matrix products, arithmetic and copies ran while one was open for 8% of the time, Pallas kernels for 0%

profile of v1, /device:TPU:0, one launch (start us, length us, event | category | flops | bytes accessed | tf_op | source)
XLA Modules:
  0.0 571.0 jit_solution(15752521169432833405)
XLA Ops:
  8.1 1.7 convolution_convert_fusion.6
  9.9 1.8 convolution_convert_fusion.7
  12.0 2.4 fusion.19
  15.5 1.6 fusion.77
  17.8 1.5 copy-done.2
  20.3 1.8 fusion.81
  22.2 84.7 %all-reduce.5.cloned.1.call-done = f32[640,768]{1,0:T(8,128)} async-done(((f32[640,768]{1,0:T(8,128)}), f32[640,768]{1,0:T(8,128)}) %all-reduce.5.cloned.1.call-update) | async-done | bytes 1966096 | tf_op jit(solution)/shard_map/psum | solution.py:99
  106.9 2.1 fusion.75
  109.7 6.5 %multiply_convert_fusion.1 = (bf16[640,768]{1,0:T(8,128)(2,1)S(1)}, f32[640,768]{1,0:T(8,128)}, f32[640,768]{1,0:T(8,128)}) fusion(f32[768]{0:T(1024)S(1)} %copy-done.34, bf16[768,768]{1,0:T(8,128)(2,1)S(1)} %copy-done, f32[640,768]{1,0:T(8,128)S(1)} %get-tuple-element.72, f32[768]{0:T(1024)S(1)} %copy-done.29, f32[768]{0:T(1024)S(1)} %copy-done.25, ...), kind=kOutput, calls=%fused_computation.32 | convolution fusion | flops 789872640 | bytes 8075264 | tf_op jit(solution)/shard_map/dot_general | solution.py:36
  117.2 1.9 convolution_convert_fusion.1
  119.1 11.8 %all-reduce.9.cloned.1.call-start = ((), (), s32[]{:S(2)}) async-start(), calls=%async_computation.9 | async-start | bytes 1966080 | tf_op jit(solution)/shard_map/psum | solution.py:119
  130.9 37.2 %all-reduce.7.cloned.1.call-done = bf16[640,768]{1,0:T(8,128)(2,1)} async-done(((bf16[640,768]{1,0:T(8,128)(2,1)}), bf16[640,768]{1,0:T(8,128)(2,1)}) %all-reduce.7.cloned.1.call-update) | async-done | bytes 983056 | tf_op jit(solution)/shard_map/psum | solution.py:106
  168.1 1.9 fusion.73
  172.2 1.8 fusion.72
  175.1 1.5 fusion.80
  177.6 1.9 convolution_convert_fusion
  179.6 49.1 %all-reduce.9.cloned.1.call-done = bf16[640,768]{1,0:T(8,128)(2,1)} async-done(((bf16[640,768]{1,0:T(8,128)(2,1)}), bf16[640,768]{1,0:T(8,128)(2,1)}) %all-reduce.9.cloned.1.call-update) | async-done | bytes 983056 | tf_op jit(solution)/shard_map/psum | solution.py:119
  228.7 3.1 multiply_reduce_fusion.1
  231.8 2.9 fusion.71
  235.0 1.4 copy-done.5
  237.8 3.1 fusion.82
  240.9 9.7 %fusion.21 = f32[3,64,640]{2,1,0:T(8,128)} fusion(pred[640]{0:T(1024)(128)(4,1)S(1)} %compare_reduce_fusion, f32[3,640,640]{1,2,0:T(8,128)} %fusion.82, f32[3,640,640]{1,2,0:T(8,128)} %copy-done.2, f32[3,640]{1,0:T(4,128)S(1)} %log_add_fusion, bf16[640,3,64]{0,2,1:T(8,128)(2,1)S(1)} %bitcast.124, bf16[640,3,64]{0,2,1:T(8,128)(2,1)S(1)} %bitcast.122), kind=kOutput, calls=%fused_computation.69 | convolution fusion | flops 167242240 | bytes 10821760 | tf_op jit(solution)/shard_map/ghqk,gqhc->gkhc/dot_general | solution.py:149
  250.6 9.6 %convolution_bitcast_fusion.4 = bf16[1,3,64,640]{3,2,1,0:T(8,128)(2,1)} fusion(bf16[640,3,64]{0,2,1:T(8,128)(2,1)S(1)} %bitcast.106, pred[640]{0:T(1024)(128)(4,1)S(1)} %compare_reduce_fusion, f32[3,640,640]{1,2,0:T(8,128)} %fusion.82, f32[3,640,640]{1,2,0:T(8,128)} %copy-done.2, f32[3,640]{1,0:T(4,128)S(1)} %log_add_fusion), kind=kOutput, calls=%fused_computation.60 | convolution fusion | flops 167119360 | bytes 10330240 | tf_op jit(solution)/shard_map/ghqk,gkhc->gqhc/dot_general | solution.py:146
  260.2 1.7 fusion.84
  261.9 9.1 %fusion.20 = bf16[3,64,640]{2,1,0:T(8,128)(2,1)S(1)} fusion(f32[3,64,640]{2,1,0:T(8,128)} %fusion.21, pred[640]{0:T(1024)(128)(4,1)S(1)} %compare_reduce_fusion, f32[3,640,640]{1,2,0:T(8,128)} %fusion.82, f32[3,640,640]{1,2,0:T(8,128)} %copy-done.2, f32[3,640]{1,0:T(4,128)S(1)} %log_add_fusion, bf16[640,3,64]{0,2,1:T(8,128)(2,1)} %bitcast.120, ...), kind=kOutput, calls=%fused_computation.63 | convolution fusion | flops 167488000 | bytes 11067520 | tf_op jit(solution)/shard_map/ghqk,gqhc->gkhc/dot_general | solution.py:151
  271.0 10.0 %select_convert_fusion.3 = (bf16[1,3,64,640]{3,2,1,0:T(8,128)(2,1)S(1)}, bf16[1,3,64,640]{3,2,1,0:T(8,128)(2,1)}, bf16[1,3,64,640]{3,2,1,0:T(8,128)(2,1)}, bf16[1,3,64,640]{3,2,1,0:T(8,128)(2,1)}) fusion(pred[640]{0:T(1024)(128)(4,1)S(1)} %compare_reduce_fusion, bf16[1,3,64,640]{3,2,1,0:T(8,128)(2,1)} %convolution_bitcast_fusion.4, ...), kind=kOutput, calls=%fused_computation.80 | convolution fusion | flops 167610880 | bytes 11313280 | tf_op jit(solution)/shard_map/ghqk,gkhc->gqhc/dot_general | solution.py:143
  282.7 3.4 fusion.12
  286.3 3.2 convolution_bitcast_fusion.1
  289.5 3.9 convolution_bitcast_fusion
  293.4 4.5 copy.56
  297.9 4.7 reshape.292
  304.0 2.2 copy.60
  306.3 2.2 convolution_bitcast_fusion.3
  308.4 2.3 copy.58
  310.8 4.2 fusion.64
  316.3 2.8 fusion.44
  319.1 1.9 constant_dynamic-update-slice_fusion.5
  321.0 1.6 collective-permute-start
  322.6 6.2 %collective-permute-done = bf16[160,768]{1,0:T(8,128)(2,1)S(1)} collective-permute-done((bf16[160,768]{1,0:T(8,128)(2,1)S(1)}, bf16[160,768]{1,0:T(8,128)(2,1)S(1)}, u32[]{:S(2)}, u32[]{:S(2)}) %collective-permute-start) | collective-permute-done | bytes 245792 | tf_op jit(solution)/shard_map/ppermute | solution.py:16
  330.0 23.7 %all-reduce = (f32[768]{0:T(1024)}, f32[768]{0:T(1024)}, f32[768]{0:T(1024)}, f32[768]{0:T(1024)}, f32[768]{0:T(1024)}, /*index=5*/f32[768]{0:T(1024)}, f32[768]{0:T(1024)}) all-reduce(f32[768]{0:T(1024)S(1)} %get-tuple-element.59, f32[768]{0:T(1024)S(1)} %get-tuple-element.45, ...), channel_id=1, replica_groups=mesh['dp'=8,'mp'=4] {'dp'}, use_global_device_ids=true, to_apply=%region_20.21 | all-reduce | flops 5376 | bytes 43008 | tf_op jit(solution)/shard_map/psum | solution.py:192
  353.7 1.6 copy.63
  359.2 2.4 constant_dynamic-slice_fusion
  361.6 32.4 %reduce-scatter.22.cloned.1.call-done = f32[96,768]{1,0:T(8,128)} async-done(((f32[768,768]{1,0:T(8,128)}), f32[96,768]{1,0:T(8,128)}) %reduce-scatter.22.cloned.1.call-update) | async-done | bytes 294928
  394.0 1.2 reshape.293
  396.1 36.6 %reduce-scatter.26.cloned.1.call-done = f32[96,192]{1,0:T(8,128)} async-done(((f32[768,192]{1,0:T(8,128)}), f32[96,192]{1,0:T(8,128)}) %reduce-scatter.26.cloned.1.call-update) | async-done | bytes 73744
  432.7 38.7 %reduce-scatter.24.cloned.1.call-done = f32[96,192]{1,0:T(8,128)} async-done(((f32[768,192]{1,0:T(8,128)}), f32[96,192]{1,0:T(8,128)}) %reduce-scatter.24.cloned.1.call-update) | async-done | bytes 73744
  471.4 46.3 %reduce-scatter.20.cloned.1.call-done = f32[768,96]{0,1:T(8,128)} async-done(((f32[768,768]{0,1:T(8,128)}), f32[768,96]{0,1:T(8,128)}) %reduce-scatter.20.cloned.1.call-update) | async-done | bytes 294928 | tf_op jit(solution)/shard_map/reduce_scatter | solution.py:190
  517.7 46.1 %reduce-scatter.18.cloned.1.call-done = f32[96,768]{1,0:T(8,128)} async-done(((f32[768,768]{1,0:T(8,128)}), f32[96,768]{1,0:T(8,128)}) %reduce-scatter.18.cloned.1.call-update) | async-done | bytes 294928 | tf_op jit(solution)/shard_map/reduce_scatter | solution.py:189
  (145 shorter events, 21.7 us)
Async XLA Ops:
  7.2 102.2 %copy-start = (bf16[768,768]{1,0:T(8,128)(2,1)S(1)}, bf16[768,768]{1,0:T(8,128)(2,1)}, u32[]{:S(2)}) copy-start(bf16[768,768]{1,0:T(8,128)(2,1)} %param.27) | copy-start | bytes 3538948
  7.2 4.8 copy-start.3
  7.2 4.5 copy-start.31
  7.2 99.6 %all-reduce.5.cloned.1.call-start = ((), (), s32[]{:S(2)}) async-start(), calls=%async_computation.7 | async-start | bytes 3932160 | tf_op jit(solution)/shard_map/psum | solution.py:99
  9.8 5.6 copy-start.8
  11.7 6.1 %copy-start.11 = (bf16[640,192]{0,1:T(8,128)(2,1)}, bf16[640,192]{0,1:T(8,128)(2,1)S(1)}, u32[]{:S(2)}) copy-start(bf16[640,192]{0,1:T(8,128)(2,1)S(1)} %convolution_convert_fusion.7) | copy-start | bytes 737284
  17.1 2.2 copy-start.2
  20.2 1.9 copy-start.10
  20.3 86.6 %copy-start.27 = (f32[768]{0:T(1024)S(1)}, f32[768]{0:T(1024)}, u32[]{:S(2)}) copy-start(f32[768]{0:T(1024)} %param.24) | copy-start | bytes 9220
  22.1 146.0 %all-reduce.7.cloned.1.call-start = ((), (), s32[]{:S(2)}) async-start(), calls=%async_computation.8 | async-start | bytes 1966080 | tf_op jit(solution)/shard_map/psum | solution.py:106
  109.7 7.5 %copy-start.32 = (bf16[768,768]{1,0:T(8,128)(2,1)S(1)}, bf16[768,768]{1,0:T(8,128)(2,1)}, u32[]{:S(2)}) copy-start(bf16[768,768]{1,0:T(8,128)(2,1)} %param.29) | copy-start | bytes 3538948
  116.2 1.0 copy-start.38
  117.2 50.9 %copy-start.28 = (f32[768]{0:T(1024)S(1)}, f32[768]{0:T(1024)}, u32[]{:S(2)}) copy-start(f32[768]{0:T(1024)} %param.30) | copy-start | bytes 9220
  119.1 109.6 %all-reduce.9.cloned.1.call-start = ((), (), s32[]{:S(2)}) async-start(), calls=%async_computation.9 | async-start | bytes 1966080 | tf_op jit(solution)/shard_map/psum | solution.py:119
  170.1 1.2 copy-start.7
  170.1 1.2 copy-start.26
  170.4 1.7 copy-start.30
  172.1 1.9 copy-start.33
  172.2 2.0 copy-start.42
  172.2 2.9 copy-start.43
  174.0 2.6 copy-start.6
  179.5 139.6 %reduce-scatter.16.cloned.1.call-start = ((), (), s32[]{:S(2)}) async-start(), calls=%async_computation.10 | async-start | bytes 1228800 | tf_op jit(solution)/shard_map/reduce_scatter | solution.py:174
  228.7 8.1 %slice-start = ((s8[4915200]{0:T(1024)(128)(4,1)}), s8[4194304]{0:T(1024)(128)(4,1)S(1)}, s32[]{:S(2)}) async-start(s8[4915200]{0:T(1024)(128)(4,1)} %bitcast.99), calls=%async_computation.17 | async-start | bytes 8388608
  231.8 5.1 slice-start.1
  234.9 1.4 copy-start.5
  237.8 3.1 copy-start.22
  237.8 3.1 copy-start.24
  240.9 9.7 %copy-start.9 = (bf16[640,192]{0,1:T(8,128)(2,1)S(1)}, bf16[640,192]{0,1:T(8,128)(2,1)}, u32[]{:S(2)}) copy-start(bf16[640,192]{0,1:T(8,128)(2,1)} %copy-done.8) | copy-start | bytes 737284
  250.6 9.6 %copy-start.15 = (bf16[768,192]{0,1:T(8,128)(2,1)S(1)}, bf16[768,192]{0,1:T(8,128)(2,1)}, u32[]{:S(2)}) copy-start(bf16[768,192]{0,1:T(8,128)(2,1)} %param.22) | copy-start | bytes 884740
  260.2 1.7 copy-start.19
  271.0 10.0 %copy-start.17 = (bf16[3,64,640]{2,1,0:T(8,128)(2,1)}, bf16[3,64,640]{2,1,0:T(8,128)(2,1)S(1)}, u32[]{:S(2)}) copy-start(bf16[3,64,640]{2,1,0:T(8,128)(2,1)S(1)} %fusion.20) | copy-start | bytes 737284
  271.0 10.0 %copy-start.16 = (bf16[768,192]{0,1:T(8,128)(2,1)S(1)}, bf16[768,192]{0,1:T(8,128)(2,1)}, u32[]{:S(2)}) copy-start(bf16[768,192]{0,1:T(8,128)(2,1)} %param.21) | copy-start | bytes 884740
  281.0 5.1 copy-start.35
  281.0 1.6 copy-start.13
  281.0 1.6 copy-start.36
  281.0 1.7 copy-start.37
  286.2 3.3 copy-start.4
  286.2 67.5 %reduce-scatter.28.cloned.1.call-start = ((), (), s32[]{:S(2)}) async-start(), calls=%async_computation.16 | async-start | bytes 884736
  289.5 104.5 %reduce-scatter.22.cloned.1.call-start = ((), (), s32[]{:S(2)}) async-start(), calls=%async_computation.13 | async-start | bytes 2654208
  302.7 130.0 %reduce-scatter.26.cloned.1.call-start = ((), (), s32[]{:S(2)}) async-start(), calls=%async_computation.15 | async-start | bytes 884736
  306.2 165.1 %reduce-scatter.24.cloned.1.call-start = ((), (), s32[]{:S(2)}) async-start(), calls=%async_computation.14 | async-start | bytes 884736
  308.4 2.4 copy-start.39
  310.8 206.9 %reduce-scatter.20.cloned.1.call-start = ((), (), s32[]{:S(2)}) async-start(), calls=%async_computation.12 | async-start | bytes 2654208 | tf_op jit(solution)/shard_map/reduce_scatter | solution.py:190
  315.1 1.2 copy-start.41
  315.1 248.7 %reduce-scatter.18.cloned.1.call-start = ((), (), s32[]{:S(2)}) async-start(), calls=%async_computation.11 | async-start | bytes 2654208 | tf_op jit(solution)/shard_map/reduce_scatter | solution.py:189
  321.0 7.8 %collective-permute-start = (bf16[160,768]{1,0:T(8,128)(2,1)S(1)}, bf16[160,768]{1,0:T(8,128)(2,1)S(1)}, u32[]{:S(2)}, u32[]{:S(2)}) collective-permute-start(bf16[160,768]{1,0:T(8,128)(2,1)S(1)} %get-tuple-element.62), channel_id=1, source_target_pairs={{0,3},{1,0},{2,1},{3,2},{4,7},{5,4},{6,5},{7,6},{8,11},{9,8},{10,9... | collective-permute-start | bytes 737288 | tf_op jit(solution)/shard_map/ppermute | solution.py:16
  328.8 27.2 %collective-permute-start.1 = (bf16[320,768]{1,0:T(8,128)(2,1)S(1)}, bf16[320,768]{1,0:T(8,128)(2,1)S(1)}, u32[]{:S(2)}, u32[]{:S(2)}) collective-permute-start(bf16[320,768]{1,0:T(8,128)(2,1)S(1)} %pad_maximum_fusion.1), channel_id=1, source_target_pairs={{0,2},{1,3},{2,0},{3,1},{4,6},{5,7},{6,4},{7,5},{8,10},{9,11},{10,... | collective-permute-start | bytes 1474568 | tf_op jit(solution)/shard_map/ppermute | solution.py:16
  358.4 205.4 %copy-start.1 = (bf16[768,768]{1,0:T(8,128)(2,1)S(1)}, bf16[768,768]{1,0:T(8,128)(2,1)}, u32[]{:S(2)}) copy-start(bf16[768,768]{1,0:T(8,128)(2,1)} %param.27) | copy-start | bytes 3538948
  (10 other events, 8.6 us)
Sparse Core Ops, SparseCore 0:
  22.2 84.5 all-reduce.4
  119.2 48.8 all-reduce.6
  179.6 49.0 all-reduce.8
  286.3 25.4 reduce-scatter.15
  314.8 33.5 reduce-scatter.27
  351.6 42.3 reduce-scatter.21
  397.7 34.9 reduce-scatter.25
  436.4 34.9 reduce-scatter.23
  475.3 42.3 reduce-scatter.19
  521.4 42.3 reduce-scatter.17
